TPU v7x, 128 devices: a whole 4x4x4 slice. The times are simulated.
128 devices in a mesh: blk: 8 (over z, y_hi), rows: 16 (over x, y_lo, core).
Axes of the slice: x: 4, y: 4 (y_hi: 2, y_lo: 2; y = y_hi * 2 + y_lo), z: 4, core: 2. Of those that a mesh axis runs over, the one named last changes fastest.
Arguments:
- embeddings: bfloat16 [65536, 768], P(('blk', 'rows')), as said below
- centroids: bfloat16 [8192, 768], P('blk'), as said below
- log_mix: float32 [8192], P('blk'), may hold values from -1.5 to 3.7
Outputs:
- new_centroids: float32 [8192, 768], P('blk')
- new_weights: float32 [8192], P('blk')
Inputs may be any that keep to these rules, and one draw needn't show every extreme that they name: `embeddings`: real vectors of no fixed length. `centroids`: real vectors of no fixed length.
All inputs are finite; a program needn't handle non-finite values.
Results may differ from a plain program's by a relative error of at most 0.0024.
Values may be sent and summed in bfloat16 or wider, within the bound.
A program may use at most 64 MiB of HBM per device.

v0:
```python
import math
import jax
import jax.numpy as jnp
from jax import lax
from jax.sharding import PartitionSpec as P

K = 8192
concentration = 32.0


def sent_to_all(x, axis):
    count = lax.axis_size(axis)
    return lax.all_to_all(jnp.broadcast_to(x[None], (count, *x.shape)), axis, 0, 0, tiled=True)


def of_everyone(x, axis):
    everything = sent_to_all(x, axis)
    return jnp.sum(everything, axis=0)


def split_up(x, dim, count):
    lengths = x.shape
    pieces = x.reshape(*lengths[:dim], count, lengths[dim] // count, *lengths[dim + 1 :])
    return jnp.moveaxis(pieces, dim, 0)


def summed_on_arrival(x, axis, dim):
    pieces = split_up(x, dim, lax.axis_size(axis))
    arrived = lax.all_to_all(pieces, axis, split_axis=0, concat_axis=0, tiled=True)
    return arrived.sum(axis=0)


def side_by_side(arrays, axis, dim, along):
    widths = [math.prod(a.shape[along:]) for a in arrays]
    both = jnp.concatenate(
        [a.reshape(*a.shape[:along], w) for a, w in zip(arrays, widths)], axis=along
    )
    filled = summed_on_arrival(both, axis, dim)
    pieces = jnp.split(filled, [sum(widths[:k]) for k in range(1, len(widths))], axis=along)
    return tuple(
        (b.reshape(*filled.shape[:along], *a.shape[along:]) for a, b in zip(arrays, pieces))
    )


def side_by_side_2(arrays, axis, dim, along):
    widths = [math.prod(a.shape[along:]) for a in arrays]
    both = jnp.concatenate(
        [a.reshape(*a.shape[:along], w) for a, w in zip(arrays, widths)], axis=along
    )
    filled = lax.all_gather(both, axis, axis=dim, tiled=True)
    pieces = jnp.split(filled, [sum(widths[:k]) for k in range(1, len(widths))], axis=along)
    return tuple(
        (b.reshape(*filled.shape[:along], *a.shape[along:]) for a, b in zip(arrays, pieces))
    )


def to_unit(values):
    values = values.astype(jnp.float32)
    return (values * lax.rsqrt(jnp.sum(values * values, axis=-1, keepdims=True) + 1e-06)).astype(
        jnp.bfloat16
    )


def finish(weighted, masses, factor):
    new_centroids = weighted * lax.rsqrt(
        jnp.sum(weighted * weighted, axis=1, keepdims=True) + 1e-06
    )
    return (new_centroids, masses * factor)


def local(embeddings, centroids, log_mix):
    centroid_units = to_unit(centroids)
    row_units = to_unit(embeddings)
    gathered = lax.all_gather(row_units, "blk", axis=0, tiled=True)
    row_total = gathered.shape[0]
    block_rows = math.gcd(row_total, 512)
    grouped = gathered.reshape(row_total // block_rows, block_rows, gathered.shape[1])

    def exponents(row_block):
        cosines = lax.dot_general(
            row_block, centroid_units, (((1,), (1,)), ((), ())), preferred_element_type=jnp.float32
        )
        return jnp.exp(log_mix[None, :] + concentration * (cosines - 1.0))

    def add_block(carried, resp, row_block):
        weighted = carried[0] + lax.dot_general(
            resp, row_block, (((0,), (0,)), ((), ())), preferred_element_type=jnp.float32
        )
        masses = carried[1] + jnp.sum(resp.astype(jnp.float32), axis=0)
        return (weighted, masses)

    local_centroids = centroids.shape[0]
    start_state = (
        jnp.zeros((local_centroids, centroids.shape[1]), jnp.float32),
        jnp.zeros((local_centroids,), jnp.float32),
    )
    partial_sums = lax.map(lambda row_block: jnp.sum(exponents(row_block), axis=1), grouped)
    totals = of_everyone(partial_sums, "blk")

    def accumulate(carried, element):
        row_block, block_totals = element
        resp = (exponents(row_block) / block_totals[:, None]).astype(jnp.bfloat16)
        return (add_block(carried, resp, row_block), None)

    (weighted, masses), _ = lax.scan(accumulate, start_state, (grouped, totals))
    factor = K / (row_total * lax.axis_size("rows"))
    share, share_masses = side_by_side((weighted, masses), "rows", 0, 1)
    new_share, weight_share = finish(share, share_masses, factor)
    return side_by_side_2((new_share, weight_share), "rows", 0, 1)


def solution(mesh):
    return jax.shard_map(
        local,
        mesh=mesh,
        in_specs=(P(("blk", "rows"), None), P("blk", None), P("blk")),
        out_specs=(P("blk", None), P("blk")),
        check_vma=False,
    )
```

profile of v0, /device:TPU:1, one launch (start us, length us, event | category | flops | bytes accessed | tf_op | source)
XLA Modules:
  0.0 282.0 jit_solution(1519887824641105736)
XLA Ops:
  11.7 90.6 %all-gather.3.cloned.1.call-done = bf16[4096,768]{1,0:T(8,128)(2,1)} async-done(((bf16[512,768]{1,0:T(8,128)(2,1)}), bf16[4096,768]{1,0:T(8,128)(2,1)}) %all-gather.3.cloned.1.call-update) | async-done | bytes 6291472 | tf_op jit(solution)/shard_map/all_gather | solution.py:74
  102.3 19.3 %while.27 = (s32[]{:T(128)}, f32[8,512]{1,0:T(8,128)S(1)}, f32[1024]{0:T(1024)S(1)}, bf16[8,512,768]{2,1,0:T(8,128)(2,1)}, bf16[1024,768]{1,0:T(8,128)(2,1)S(1)}, /*index=5*/s32[]{:T(128)}, s32[]{:T(128)}) while((s32[]{:T(128)}, f32[8,512]{1,0:T(8,128)S(1)}, f32[1024]{0:T(1024)S(1)}, bf16[8,512,768]{2,1,0:T(8,128)(2,1)}, ...), condition=%wide.region_4.5_spmd, body=%wide.region_2.4_spmd.sunk | while | flops 807403008 | bytes 2369629 | solution.py:97
  102.3 2.3 exponential_reduce_fusion.2
  104.7 2.3 exponential_reduce_fusion.2
  107.1 2.3 exponential_reduce_fusion.2
  109.6 2.3 exponential_reduce_fusion.2
  112.0 2.3 exponential_reduce_fusion.2
  114.4 2.3 exponential_reduce_fusion.2
  116.8 2.3 exponential_reduce_fusion.2
  119.2 2.3 exponential_reduce_fusion.2
  122.3 3.4 %all-to-all-start = ((f32[8,8,512]{2,1,0:T(8,128)}), f32[8,8,512]{2,1,0:T(8,128)S(1)}, u32[]{:S(2)}, u32[]{:S(2)}) async-start(f32[8,8,512]{2,1,0:T(8,128)} %broadcast_in_dim.31), calls=%async_computation | async-start | bytes 262144 | tf_op jit(solution)/shard_map/all_to_all | solution.py:13
  125.8 6.9 %all-to-all-done = f32[8,8,512]{2,1,0:T(8,128)S(1)} async-done(((f32[8,8,512]{2,1,0:T(8,128)}), f32[8,8,512]{2,1,0:T(8,128)S(1)}, u32[]{:S(2)}, u32[]{:S(2)}) %all-to-all-start) | async-done | bytes 131104 | tf_op jit(solution)/shard_map/all_to_all | solution.py:13
  132.7 47.6 %while.28 = (s32[]{:T(128)}, f32[1024,768]{1,0:T(8,128)S(1)}, f32[1024]{0:T(1024)S(1)}, f32[1024]{0:T(1024)S(1)}, bf16[8,512,768]{2,1,0:T(8,128)(2,1)}, /*index=...) while((s32[]{:T(128)}, f32[1024,768]{1,0:T(8,128)S(1)}, ...), condition=%wide.region_8.9_spmd.clone, body=%wide.region_6.8_spmd.clone.sunk | while | flops 1615856640 | bytes 11561084 | solution.py:105
  132.7 2.9 %convert_reduce_fusion.2 = (f32[1024]{0:T(1024)S(1)}, bf16[512,1024]{1,0:T(8,128)(2,1)S(1)}) fusion(f32[512]{0:T(512)S(1)} %bitcast.36, bf16[1024,768]{1,0:T(8,128)(2,1)} %get-tuple-element.332, bf16[8,512,768]{2,1,0:T(8,128)(2,1)} %get-tuple-element.331, s32[]{:T(128)S(6)} %copy.17, f32[1024]{0:T(1024)S(1)} %get-tuple-element.330), kind=kOutput, calls=%fused_computation.5.clone.1 | convolution fusion | flops 808975360 | bytes 3418116 | tf_op jit(solution)/shard_map/while/body/eval_jaxpr/dot_general | solution.py:80
  135.6 3.0 %select_add_fusion.4 = f32[1024,768]{1,0:T(8,128)S(1)} fusion(f32[1024,768]{1,0:T(8,128)S(1)} %get-tuple-element.319, bf16[512,1024]{1,0:T(8,128)(2,1)S(1)} %get-tuple-element.286, pred[]{:T(512)S(6)} %compare.3, bf16[8,512,768]{2,1,0:T(8,128)(2,1)} %get-tuple-element.331, s32[]{:T(128)S(6)} %copy.17), kind=kOutput, calls=%fused_computation.4.clone.1 | convolution fusion | flops 806879232 | bytes 8126469 | tf_op jit(solution)/shard_map/while/body/eval_jaxpr/dot_general | solution.py:86
  138.7 2.9 %convert_reduce_fusion.2 = (f32[1024]{0:T(1024)S(1)}, bf16[512,1024]{1,0:T(8,128)(2,1)S(1)}) fusion(f32[512]{0:T(512)S(1)} %bitcast.36, bf16[1024,768]{1,0:T(8,128)(2,1)} %get-tuple-element.332, bf16[8,512,768]{2,1,0:T(8,128)(2,1)} %get-tuple-element.331, s32[]{:T(128)S(6)} %copy.17, f32[1024]{0:T(1024)S(1)} %get-tuple-element.330), kind=kOutput, calls=%fused_computation.5.clone.1 | convolution fusion | flops 808975360 | bytes 3418116 | tf_op jit(solution)/shard_map/while/body/eval_jaxpr/dot_general | solution.py:80
  141.6 3.0 %select_add_fusion.4 = f32[1024,768]{1,0:T(8,128)S(1)} fusion(f32[1024,768]{1,0:T(8,128)S(1)} %get-tuple-element.319, bf16[512,1024]{1,0:T(8,128)(2,1)S(1)} %get-tuple-element.286, pred[]{:T(512)S(6)} %compare.3, bf16[8,512,768]{2,1,0:T(8,128)(2,1)} %get-tuple-element.331, s32[]{:T(128)S(6)} %copy.17), kind=kOutput, calls=%fused_computation.4.clone.1 | convolution fusion | flops 806879232 | bytes 8126469 | tf_op jit(solution)/shard_map/while/body/eval_jaxpr/dot_general | solution.py:86
  144.6 2.9 %convert_reduce_fusion.2 = (f32[1024]{0:T(1024)S(1)}, bf16[512,1024]{1,0:T(8,128)(2,1)S(1)}) fusion(f32[512]{0:T(512)S(1)} %bitcast.36, bf16[1024,768]{1,0:T(8,128)(2,1)} %get-tuple-element.332, bf16[8,512,768]{2,1,0:T(8,128)(2,1)} %get-tuple-element.331, s32[]{:T(128)S(6)} %copy.17, f32[1024]{0:T(1024)S(1)} %get-tuple-element.330), kind=kOutput, calls=%fused_computation.5.clone.1 | convolution fusion | flops 808975360 | bytes 3418116 | tf_op jit(solution)/shard_map/while/body/eval_jaxpr/dot_general | solution.py:80
  147.5 3.0 %select_add_fusion.4 = f32[1024,768]{1,0:T(8,128)S(1)} fusion(f32[1024,768]{1,0:T(8,128)S(1)} %get-tuple-element.319, bf16[512,1024]{1,0:T(8,128)(2,1)S(1)} %get-tuple-element.286, pred[]{:T(512)S(6)} %compare.3, bf16[8,512,768]{2,1,0:T(8,128)(2,1)} %get-tuple-element.331, s32[]{:T(128)S(6)} %copy.17), kind=kOutput, calls=%fused_computation.4.clone.1 | convolution fusion | flops 806879232 | bytes 8126469 | tf_op jit(solution)/shard_map/while/body/eval_jaxpr/dot_general | solution.py:86
  150.6 2.9 %convert_reduce_fusion.2 = (f32[1024]{0:T(1024)S(1)}, bf16[512,1024]{1,0:T(8,128)(2,1)S(1)}) fusion(f32[512]{0:T(512)S(1)} %bitcast.36, bf16[1024,768]{1,0:T(8,128)(2,1)} %get-tuple-element.332, bf16[8,512,768]{2,1,0:T(8,128)(2,1)} %get-tuple-element.331, s32[]{:T(128)S(6)} %copy.17, f32[1024]{0:T(1024)S(1)} %get-tuple-element.330), kind=kOutput, calls=%fused_computation.5.clone.1 | convolution fusion | flops 808975360 | bytes 3418116 | tf_op jit(solution)/shard_map/while/body/eval_jaxpr/dot_general | solution.py:80
  153.5 3.0 %select_add_fusion.4 = f32[1024,768]{1,0:T(8,128)S(1)} fusion(f32[1024,768]{1,0:T(8,128)S(1)} %get-tuple-element.319, bf16[512,1024]{1,0:T(8,128)(2,1)S(1)} %get-tuple-element.286, pred[]{:T(512)S(6)} %compare.3, bf16[8,512,768]{2,1,0:T(8,128)(2,1)} %get-tuple-element.331, s32[]{:T(128)S(6)} %copy.17), kind=kOutput, calls=%fused_computation.4.clone.1 | convolution fusion | flops 806879232 | bytes 8126469 | tf_op jit(solution)/shard_map/while/body/eval_jaxpr/dot_general | solution.py:86
  156.5 2.9 %convert_reduce_fusion.2 = (f32[1024]{0:T(1024)S(1)}, bf16[512,1024]{1,0:T(8,128)(2,1)S(1)}) fusion(f32[512]{0:T(512)S(1)} %bitcast.36, bf16[1024,768]{1,0:T(8,128)(2,1)} %get-tuple-element.332, bf16[8,512,768]{2,1,0:T(8,128)(2,1)} %get-tuple-element.331, s32[]{:T(128)S(6)} %copy.17, f32[1024]{0:T(1024)S(1)} %get-tuple-element.330), kind=kOutput, calls=%fused_computation.5.clone.1 | convolution fusion | flops 808975360 | bytes 3418116 | tf_op jit(solution)/shard_map/while/body/eval_jaxpr/dot_general | solution.py:80
  159.4 3.0 %select_add_fusion.4 = f32[1024,768]{1,0:T(8,128)S(1)} fusion(f32[1024,768]{1,0:T(8,128)S(1)} %get-tuple-element.319, bf16[512,1024]{1,0:T(8,128)(2,1)S(1)} %get-tuple-element.286, pred[]{:T(512)S(6)} %compare.3, bf16[8,512,768]{2,1,0:T(8,128)(2,1)} %get-tuple-element.331, s32[]{:T(128)S(6)} %copy.17), kind=kOutput, calls=%fused_computation.4.clone.1 | convolution fusion | flops 806879232 | bytes 8126469 | tf_op jit(solution)/shard_map/while/body/eval_jaxpr/dot_general | solution.py:86
  162.5 2.9 %convert_reduce_fusion.2 = (f32[1024]{0:T(1024)S(1)}, bf16[512,1024]{1,0:T(8,128)(2,1)S(1)}) fusion(f32[512]{0:T(512)S(1)} %bitcast.36, bf16[1024,768]{1,0:T(8,128)(2,1)} %get-tuple-element.332, bf16[8,512,768]{2,1,0:T(8,128)(2,1)} %get-tuple-element.331, s32[]{:T(128)S(6)} %copy.17, f32[1024]{0:T(1024)S(1)} %get-tuple-element.330), kind=kOutput, calls=%fused_computation.5.clone.1 | convolution fusion | flops 808975360 | bytes 3418116 | tf_op jit(solution)/shard_map/while/body/eval_jaxpr/dot_general | solution.py:80
  165.4 3.0 %select_add_fusion.4 = f32[1024,768]{1,0:T(8,128)S(1)} fusion(f32[1024,768]{1,0:T(8,128)S(1)} %get-tuple-element.319, bf16[512,1024]{1,0:T(8,128)(2,1)S(1)} %get-tuple-element.286, pred[]{:T(512)S(6)} %compare.3, bf16[8,512,768]{2,1,0:T(8,128)(2,1)} %get-tuple-element.331, s32[]{:T(128)S(6)} %copy.17), kind=kOutput, calls=%fused_computation.4.clone.1 | convolution fusion | flops 806879232 | bytes 8126469 | tf_op jit(solution)/shard_map/while/body/eval_jaxpr/dot_general | solution.py:86
  168.4 2.9 %convert_reduce_fusion.2 = (f32[1024]{0:T(1024)S(1)}, bf16[512,1024]{1,0:T(8,128)(2,1)S(1)}) fusion(f32[512]{0:T(512)S(1)} %bitcast.36, bf16[1024,768]{1,0:T(8,128)(2,1)} %get-tuple-element.332, bf16[8,512,768]{2,1,0:T(8,128)(2,1)} %get-tuple-element.331, s32[]{:T(128)S(6)} %copy.17, f32[1024]{0:T(1024)S(1)} %get-tuple-element.330), kind=kOutput, calls=%fused_computation.5.clone.1 | convolution fusion | flops 808975360 | bytes 3418116 | tf_op jit(solution)/shard_map/while/body/eval_jaxpr/dot_general | solution.py:80
  171.4 3.0 %select_add_fusion.4 = f32[1024,768]{1,0:T(8,128)S(1)} fusion(f32[1024,768]{1,0:T(8,128)S(1)} %get-tuple-element.319, bf16[512,1024]{1,0:T(8,128)(2,1)S(1)} %get-tuple-element.286, pred[]{:T(512)S(6)} %compare.3, bf16[8,512,768]{2,1,0:T(8,128)(2,1)} %get-tuple-element.331, s32[]{:T(128)S(6)} %copy.17), kind=kOutput, calls=%fused_computation.4.clone.1 | convolution fusion | flops 806879232 | bytes 8126469 | tf_op jit(solution)/shard_map/while/body/eval_jaxpr/dot_general | solution.py:86
  174.4 2.9 %convert_reduce_fusion.2 = (f32[1024]{0:T(1024)S(1)}, bf16[512,1024]{1,0:T(8,128)(2,1)S(1)}) fusion(f32[512]{0:T(512)S(1)} %bitcast.36, bf16[1024,768]{1,0:T(8,128)(2,1)} %get-tuple-element.332, bf16[8,512,768]{2,1,0:T(8,128)(2,1)} %get-tuple-element.331, s32[]{:T(128)S(6)} %copy.17, f32[1024]{0:T(1024)S(1)} %get-tuple-element.330), kind=kOutput, calls=%fused_computation.5.clone.1 | convolution fusion | flops 808975360 | bytes 3418116 | tf_op jit(solution)/shard_map/while/body/eval_jaxpr/dot_general | solution.py:80
  177.3 3.0 %select_add_fusion.4 = f32[1024,768]{1,0:T(8,128)S(1)} fusion(f32[1024,768]{1,0:T(8,128)S(1)} %get-tuple-element.319, bf16[512,1024]{1,0:T(8,128)(2,1)S(1)} %get-tuple-element.286, pred[]{:T(512)S(6)} %compare.3, bf16[8,512,768]{2,1,0:T(8,128)(2,1)} %get-tuple-element.331, s32[]{:T(128)S(6)} %copy.17), kind=kOutput, calls=%fused_computation.4.clone.1 | convolution fusion | flops 806879232 | bytes 8126469 | tf_op jit(solution)/shard_map/while/body/eval_jaxpr/dot_general | solution.py:86
  182.8 50.4 %all_to_all.10 = f32[16,64,769]{2,1,0:T(8,128)} all-to-all(f32[16,64,769]{2,1,0:T(8,128)S(1)} %pad_maximum_fusion), channel_id=1, replica_groups=mesh['blk'=8,'rows'=16] {'rows'}, dimensions={0} | all-to-all | bytes 6299648 | tf_op jit(solution)/shard_map/all_to_all | solution.py:29
  236.5 33.2 %all-gather.5.cloned.1.call-done = f32[1024,769]{1,0:T(8,128)} async-done(((f32[64,769]{1,0:T(8,128)}), f32[1024,769]{1,0:T(8,128)}) %all-gather.5.cloned.1.call-update) | async-done | bytes 3149840 | tf_op jit(solution)/shard_map/all_gather | solution.py:50
  271.5 3.8 %split.18 = f32[1024,768]{1,0:T(8,128)} slice(f32[1024,769]{1,0:T(8,128)} %all-gather.5.cloned.1.call-done), slice={[0:1024], [0:768]} | slice | bytes 6291456 | tf_op jit(solution)/shard_map/split | solution.py:51
  (54 shorter events, 13.3 us)
Async XLA Ops:
  7.2 3.8 %copy-start = (bf16[1024,768]{1,0:T(8,128)(2,1)S(1)}, bf16[1024,768]{1,0:T(8,128)(2,1)}, u32[]{:S(2)}) copy-start(bf16[1024,768]{1,0:T(8,128)(2,1)} %param.8) | copy-start | bytes 4718596
  7.2 95.2 %all-gather.3.cloned.1.call-start = ((), (), s32[]{:S(2)}) async-start(), calls=%async_computation.2 | async-start | bytes 7077888 | tf_op jit(solution)/shard_map/all_gather | solution.py:74
  11.0 91.4 %copy-start.2 = (f32[1024]{0:T(1024)S(1)}, f32[1024]{0:T(1024)}, u32[]{:S(2)}) copy-start(f32[1024]{0:T(1024)} %param.9) | copy-start | bytes 12292
  121.6 4.2 %copy-start.1 = (bf16[1024,768]{1,0:T(8,128)(2,1)}, bf16[1024,768]{1,0:T(8,128)(2,1)S(1)}, u32[]{:S(2)}) copy-start(bf16[1024,768]{1,0:T(8,128)(2,1)S(1)} %get-tuple-element.343) | copy-start | bytes 4718596
  122.3 10.4 %all-to-all-start = ((f32[8,8,512]{2,1,0:T(8,128)}), f32[8,8,512]{2,1,0:T(8,128)S(1)}, u32[]{:S(2)}, u32[]{:S(2)}) async-start(f32[8,8,512]{2,1,0:T(8,128)} %broadcast_in_dim.31), calls=%async_computation | async-start | bytes 262144 | tf_op jit(solution)/shard_map/all_to_all | solution.py:13
  125.7 143.9 %all-gather.5.cloned.1.call-start = ((), (), s32[]{:S(2)}) async-start(), calls=%async_computation.3 | async-start | bytes 3899392 | tf_op jit(solution)/shard_map/all_gather | solution.py:50
Sparse Core Ops, SparseCore 0:
  11.1 91.2 all-gather.2
  236.6 32.9 all-gather.4
where the time goes:
time: 283 us; the launch traced here: 282 us
  waiting for transfers between devices  131 us (46%)
  matrix products  65.8 us (23%)
  blocking collectives  50.4 us (18%)
  between operations  14.2 us (5%)
  other arithmetic  8.97 us (3%)
  local copies, waits for them, and re-layouts  7.99 us (3%)
  starting transfers between devices  3.45 us (1%)
    all_gather x1, waiting for transfers between devices, local(): gathered = lax.all_gather(row_units, 'blk', axis=0, tiled=True)  90.6 us
    all_to_all x1, blocking collectives, summed_on_arrival(): lax.all_to_all(pieces, axis, split_axis=0, concat_axis=0, tiled=True)  50.4 us
    dot_general x16, matrix products, exponents(): lax.dot_general(row_block, centroid_units, (((1,), (1,)), ((), ())), pref...  41.7 us
    all_gather x1, waiting for transfers between devices, side_by_side_2(): filled = lax.all_gather(both, axis, axis=dim, tiled=True)  33.2 us
    dot_general x8, matrix products, add_block(): lax.dot_general(resp, row_block, (((0,), (0,)), ((), ())), preferred_elem...  24 us
    all_to_all x1, waiting for transfers between devices, sent_to_all(): lax.all_to_all(jnp.broadcast_to(x[None], (count, *x.shape)), axis, 0, 0,...  6.9 us
  transfers between devices with their start and end apart: 3, of which 3 were waited for; matrix products, arithmetic and copies ran while one was open for 0% of the time, Pallas kernels for 0%

commit v1 on v0

--- a/solution.py
+++ b/solution.py
@@ -71,7 +71,12 @@
 def local(embeddings, centroids, log_mix):
     centroid_units = to_unit(centroids)
     row_units = to_unit(embeddings)
-    gathered = lax.all_gather(row_units, "blk", axis=0, tiled=True)
+    gathered = jnp.concatenate(
+        lax.all_to_all(
+            jnp.stack([row_units for _ in range(lax.axis_size("blk"))], axis=0), "blk", 0, 0
+        ),
+        axis=0,
+    )
     row_total = gathered.shape[0]
     block_rows = math.gcd(row_total, 512)
     grouped = gathered.reshape(row_total // block_rows, block_rows, gathered.shape[1])

time: 283 us -> 286 us (1.011)
  waiting for transfers between devices: 131 us -> 112 us
  matrix products: 65.8 us -> 76.1 us
  starting transfers between devices: 3.45 us -> 12.4 us
  local copies, waits for them, and re-layouts: 7.99 us -> 11 us
    all_gather x1 -> x0, waiting for transfers between devices: 90.6 us -> none  [local(): gathered = lax.all_gather(row_units, 'blk', axis=0, tiled=True)]
    all_to_all x0 -> x1, waiting for transfers between devices: none -> 71.9 us  [local(): lax.all_to_all(jnp.stack([row_units for _ in range(lax.axis_size('blk'))]...]
    all_to_all x0 -> x1, starting transfers between devices: none -> 8.61 us  [local(): lax.all_to_all(jnp.stack([row_units for _ in range(lax.axis_size('blk'))]...]
    dot_general x16, matrix products: 41.7 us -> 49.8 us  [exponents(): lax.dot_general(row_block, centroid_units, (((1,), (1,)), ((), ())), pref...]
    another operation x0 -> x1, local copies, waits for them, and re-layouts: none -> 3.06 us  [local(): jnp.stack([row_units for _ in range(lax.axis_size('blk'))], axis=0)]
where the time goes in v1:
time: 286 us; the launch traced here: 284 us
  waiting for transfers between devices  112 us (39%)
  matrix products  76.1 us (27%)
  blocking collectives  50.3 us (18%)
  between operations  14.1 us (5%)
  starting transfers between devices  12.4 us (4%)
  local copies, waits for them, and re-layouts  11 us (4%)
  other arithmetic  7.98 us (3%)
    all_to_all x1, waiting for transfers between devices, local(): lax.all_to_all(jnp.stack([row_units for _ in range(lax.axis_size('blk'))]...  71.9 us
    all_to_all x1, blocking collectives, summed_on_arrival(): lax.all_to_all(pieces, axis, split_axis=0, concat_axis=0, tiled=True)  50.3 us
    dot_general x16, matrix products, exponents(): lax.dot_general(row_block, centroid_units, (((1,), (1,)), ((), ())), pref...  49.8 us
    all_gather x1, waiting for transfers between devices, side_by_side_2(): filled = lax.all_gather(both, axis, axis=dim, tiled=True)  33.1 us
    dot_general x8, matrix products, add_block(): lax.dot_general(resp, row_block, (((0,), (0,)), ((), ())), preferred_elem...  26.4 us
    all_to_all x1, starting transfers between devices, local(): lax.all_to_all(jnp.stack([row_units for _ in range(lax.axis_size('blk'))]...  8.61 us
    all_to_all x1, waiting for transfers between devices, sent_to_all(): lax.all_to_all(jnp.broadcast_to(x[None], (count, *x.shape)), axis, 0, 0,...  6.98 us
  transfers between devices with their start and end apart: 3, of which 3 were waited for; matrix products, arithmetic and copies ran while one was open for 0% of the time, Pallas kernels for 0%

profile of v1, /device:TPU:1, one launch (start us, length us, event | category | flops | bytes accessed | tf_op | source)
XLA Modules:
  0.0 284.5 jit_solution(6106601125382068198)
XLA Ops:
  9.9 3.1 %stack.2 = bf16[8,512,768]{2,1,0:T(8,128)(2,1)} broadcast(bf16[512,768]{1,0:T(8,128)(2,1)S(1)} %fusion.12), dimensions={1,2} | broadcast | bytes 7077888 | tf_op jit(solution)/shard_map/stack | solution.py:76
  12.9 8.6 %all-to-all-start = ((bf16[8,512,768]{2,1,0:T(8,128)(2,1)}), bf16[8,512,768]{2,1,0:T(8,128)(2,1)}, u32[]{:S(2)}, u32[]{:S(2)}) async-start(bf16[8,512,768]{2,1,0:T(8,128)(2,1)} %stack.2), calls=%async_computation | async-start | bytes 12582912 | tf_op jit(solution)/shard_map/all_to_all | solution.py:75
  22.3 71.9 %all-to-all-done = bf16[8,512,768]{2,1,0:T(8,128)(2,1)} async-done(((bf16[8,512,768]{2,1,0:T(8,128)(2,1)}), bf16[8,512,768]{2,1,0:T(8,128)(2,1)}, u32[]{:S(2)}, u32[]{:S(2)}) %all-to-all-start) | async-done | bytes 6291488 | tf_op jit(solution)/shard_map/all_to_all | solution.py:75
  94.2 19.2 %while.27 = (s32[]{:T(128)}, f32[8,512]{1,0:T(8,128)S(1)}, f32[1024]{0:T(1024)S(1)}, bf16[8,512,768]{2,1,0:T(8,128)(2,1)}, bf16[1024,768]{1,0:T(8,128)(2,1)S(1)}, /*index=5*/s32[]{:T(128)}, s32[]{:T(128)}) while((s32[]{:T(128)}, f32[8,512]{1,0:T(8,128)S(1)}, f32[1024]{0:T(1024)S(1)}, bf16[8,512,768]{2,1,0:T(8,128)(2,1)}, ...), condition=%wide.region_4.5_spmd, body=%wide.region_2.4_spmd.sunk | while | flops 807403008 | bytes 2370129 | solution.py:102
  99.0 2.3 exponential_reduce_fusion.2
  101.4 2.3 exponential_reduce_fusion.2
  103.8 2.3 exponential_reduce_fusion.2
  106.2 2.3 exponential_reduce_fusion.2
  108.6 2.3 exponential_reduce_fusion.2
  111.0 2.3 exponential_reduce_fusion.2
  114.2 3.8 %all-to-all-start.1 = ((f32[8,8,512]{2,1,0:T(8,128)}), f32[8,8,512]{2,1,0:T(8,128)S(1)}, u32[]{:S(2)}, u32[]{:S(2)}) async-start(f32[8,8,512]{2,1,0:T(8,128)} %broadcast_in_dim.31), calls=%async_computation.1 | async-start | bytes 262144 | tf_op jit(solution)/shard_map/all_to_all | solution.py:13
  118.0 7.0 %all-to-all-done.1 = f32[8,8,512]{2,1,0:T(8,128)S(1)} async-done(((f32[8,8,512]{2,1,0:T(8,128)}), f32[8,8,512]{2,1,0:T(8,128)S(1)}, u32[]{:S(2)}, u32[]{:S(2)}) %all-to-all-start.1) | async-done | bytes 131104 | tf_op jit(solution)/shard_map/all_to_all | solution.py:13
  125.0 57.9 %while.28 = (s32[]{:T(128)}, f32[1024,768]{1,0:T(8,128)S(1)}, f32[1024]{0:T(1024)S(1)}, f32[1024]{0:T(1024)S(1)}, bf16[8,512,768]{2,1,0:T(8,128)(2,1)}, /*index=...) while((s32[]{:T(128)}, f32[1024,768]{1,0:T(8,128)S(1)}, ...), condition=%wide.region_8.9_spmd.clone, body=%wide.region_6.8_spmd.clone.sunk | while | flops 1615856640 | bytes 11562092 | solution.py:110
  125.0 3.9 %convert_reduce_fusion.2 = (f32[1024]{0:T(1024)S(1)}, bf16[512,1024]{1,0:T(8,128)(2,1)}) fusion(f32[512]{0:T(512)S(1)} %bitcast.34, bf16[1024,768]{1,0:T(8,128)(2,1)} %get-tuple-element.332, bf16[8,512,768]{2,1,0:T(8,128)(2,1)} %get-tuple-element.331, s32[]{:T(128)} %get-tuple-element.318, f32[1024]{0:T(1024)S(1)} %get-tuple-element.330), kind=kOutput, calls=%fused_computation.5.clone.1 | convolution fusion | flops 808975360 | bytes 3418624 | tf_op jit(solution)/shard_map/while/body/eval_jaxpr/dot_general | solution.py:85
  128.9 3.3 %select_add_fusion.4 = f32[1024,768]{1,0:T(8,128)S(1)} fusion(f32[1024,768]{1,0:T(8,128)S(1)} %get-tuple-element.319, bf16[512,1024]{1,0:T(8,128)(2,1)} %get-tuple-element.286, pred[]{:T(512)S(6)} %compare.3, bf16[8,512,768]{2,1,0:T(8,128)(2,1)} %get-tuple-element.331, s32[]{:T(128)} %get-tuple-element.318), kind=kOutput, calls=%fused_computation.4.clone.1 | convolution fusion | flops 806879232 | bytes 8126977 | tf_op jit(solution)/shard_map/while/body/eval_jaxpr/dot_general | solution.py:91
  132.3 3.9 %convert_reduce_fusion.2 = (f32[1024]{0:T(1024)S(1)}, bf16[512,1024]{1,0:T(8,128)(2,1)}) fusion(f32[512]{0:T(512)S(1)} %bitcast.34, bf16[1024,768]{1,0:T(8,128)(2,1)} %get-tuple-element.332, bf16[8,512,768]{2,1,0:T(8,128)(2,1)} %get-tuple-element.331, s32[]{:T(128)} %get-tuple-element.318, f32[1024]{0:T(1024)S(1)} %get-tuple-element.330), kind=kOutput, calls=%fused_computation.5.clone.1 | convolution fusion | flops 808975360 | bytes 3418624 | tf_op jit(solution)/shard_map/while/body/eval_jaxpr/dot_general | solution.py:85
  136.2 3.3 %select_add_fusion.4 = f32[1024,768]{1,0:T(8,128)S(1)} fusion(f32[1024,768]{1,0:T(8,128)S(1)} %get-tuple-element.319, bf16[512,1024]{1,0:T(8,128)(2,1)} %get-tuple-element.286, pred[]{:T(512)S(6)} %compare.3, bf16[8,512,768]{2,1,0:T(8,128)(2,1)} %get-tuple-element.331, s32[]{:T(128)} %get-tuple-element.318), kind=kOutput, calls=%fused_computation.4.clone.1 | convolution fusion | flops 806879232 | bytes 8126977 | tf_op jit(solution)/shard_map/while/body/eval_jaxpr/dot_general | solution.py:91
  139.5 3.9 %convert_reduce_fusion.2 = (f32[1024]{0:T(1024)S(1)}, bf16[512,1024]{1,0:T(8,128)(2,1)}) fusion(f32[512]{0:T(512)S(1)} %bitcast.34, bf16[1024,768]{1,0:T(8,128)(2,1)} %get-tuple-element.332, bf16[8,512,768]{2,1,0:T(8,128)(2,1)} %get-tuple-element.331, s32[]{:T(128)} %get-tuple-element.318, f32[1024]{0:T(1024)S(1)} %get-tuple-element.330), kind=kOutput, calls=%fused_computation.5.clone.1 | convolution fusion | flops 808975360 | bytes 3418624 | tf_op jit(solution)/shard_map/while/body/eval_jaxpr/dot_general | solution.py:85
  143.4 3.3 %select_add_fusion.4 = f32[1024,768]{1,0:T(8,128)S(1)} fusion(f32[1024,768]{1,0:T(8,128)S(1)} %get-tuple-element.319, bf16[512,1024]{1,0:T(8,128)(2,1)} %get-tuple-element.286, pred[]{:T(512)S(6)} %compare.3, bf16[8,512,768]{2,1,0:T(8,128)(2,1)} %get-tuple-element.331, s32[]{:T(128)} %get-tuple-element.318), kind=kOutput, calls=%fused_computation.4.clone.1 | convolution fusion | flops 806879232 | bytes 8126977 | tf_op jit(solution)/shard_map/while/body/eval_jaxpr/dot_general | solution.py:91
  146.8 3.9 %convert_reduce_fusion.2 = (f32[1024]{0:T(1024)S(1)}, bf16[512,1024]{1,0:T(8,128)(2,1)}) fusion(f32[512]{0:T(512)S(1)} %bitcast.34, bf16[1024,768]{1,0:T(8,128)(2,1)} %get-tuple-element.332, bf16[8,512,768]{2,1,0:T(8,128)(2,1)} %get-tuple-element.331, s32[]{:T(128)} %get-tuple-element.318, f32[1024]{0:T(1024)S(1)} %get-tuple-element.330), kind=kOutput, calls=%fused_computation.5.clone.1 | convolution fusion | flops 808975360 | bytes 3418624 | tf_op jit(solution)/shard_map/while/body/eval_jaxpr/dot_general | solution.py:85
  150.7 3.3 %select_add_fusion.4 = f32[1024,768]{1,0:T(8,128)S(1)} fusion(f32[1024,768]{1,0:T(8,128)S(1)} %get-tuple-element.319, bf16[512,1024]{1,0:T(8,128)(2,1)} %get-tuple-element.286, pred[]{:T(512)S(6)} %compare.3, bf16[8,512,768]{2,1,0:T(8,128)(2,1)} %get-tuple-element.331, s32[]{:T(128)} %get-tuple-element.318), kind=kOutput, calls=%fused_computation.4.clone.1 | convolution fusion | flops 806879232 | bytes 8126977 | tf_op jit(solution)/shard_map/while/body/eval_jaxpr/dot_general | solution.py:91
  154.0 3.9 %convert_reduce_fusion.2 = (f32[1024]{0:T(1024)S(1)}, bf16[512,1024]{1,0:T(8,128)(2,1)}) fusion(f32[512]{0:T(512)S(1)} %bitcast.34, bf16[1024,768]{1,0:T(8,128)(2,1)} %get-tuple-element.332, bf16[8,512,768]{2,1,0:T(8,128)(2,1)} %get-tuple-element.331, s32[]{:T(128)} %get-tuple-element.318, f32[1024]{0:T(1024)S(1)} %get-tuple-element.330), kind=kOutput, calls=%fused_computation.5.clone.1 | convolution fusion | flops 808975360 | bytes 3418624 | tf_op jit(solution)/shard_map/while/body/eval_jaxpr/dot_general | solution.py:85
  157.9 3.3 %select_add_fusion.4 = f32[1024,768]{1,0:T(8,128)S(1)} fusion(f32[1024,768]{1,0:T(8,128)S(1)} %get-tuple-element.319, bf16[512,1024]{1,0:T(8,128)(2,1)} %get-tuple-element.286, pred[]{:T(512)S(6)} %compare.3, bf16[8,512,768]{2,1,0:T(8,128)(2,1)} %get-tuple-element.331, s32[]{:T(128)} %get-tuple-element.318), kind=kOutput, calls=%fused_computation.4.clone.1 | convolution fusion | flops 806879232 | bytes 8126977 | tf_op jit(solution)/shard_map/while/body/eval_jaxpr/dot_general | solution.py:91
  161.2 3.9 %convert_reduce_fusion.2 = (f32[1024]{0:T(1024)S(1)}, bf16[512,1024]{1,0:T(8,128)(2,1)}) fusion(f32[512]{0:T(512)S(1)} %bitcast.34, bf16[1024,768]{1,0:T(8,128)(2,1)} %get-tuple-element.332, bf16[8,512,768]{2,1,0:T(8,128)(2,1)} %get-tuple-element.331, s32[]{:T(128)} %get-tuple-element.318, f32[1024]{0:T(1024)S(1)} %get-tuple-element.330), kind=kOutput, calls=%fused_computation.5.clone.1 | convolution fusion | flops 808975360 | bytes 3418624 | tf_op jit(solution)/shard_map/while/body/eval_jaxpr/dot_general | solution.py:85
  165.1 3.3 %select_add_fusion.4 = f32[1024,768]{1,0:T(8,128)S(1)} fusion(f32[1024,768]{1,0:T(8,128)S(1)} %get-tuple-element.319, bf16[512,1024]{1,0:T(8,128)(2,1)} %get-tuple-element.286, pred[]{:T(512)S(6)} %compare.3, bf16[8,512,768]{2,1,0:T(8,128)(2,1)} %get-tuple-element.331, s32[]{:T(128)} %get-tuple-element.318), kind=kOutput, calls=%fused_computation.4.clone.1 | convolution fusion | flops 806879232 | bytes 8126977 | tf_op jit(solution)/shard_map/while/body/eval_jaxpr/dot_general | solution.py:91
  168.5 3.9 %convert_reduce_fusion.2 = (f32[1024]{0:T(1024)S(1)}, bf16[512,1024]{1,0:T(8,128)(2,1)}) fusion(f32[512]{0:T(512)S(1)} %bitcast.34, bf16[1024,768]{1,0:T(8,128)(2,1)} %get-tuple-element.332, bf16[8,512,768]{2,1,0:T(8,128)(2,1)} %get-tuple-element.331, s32[]{:T(128)} %get-tuple-element.318, f32[1024]{0:T(1024)S(1)} %get-tuple-element.330), kind=kOutput, calls=%fused_computation.5.clone.1 | convolution fusion | flops 808975360 | bytes 3418624 | tf_op jit(solution)/shard_map/while/body/eval_jaxpr/dot_general | solution.py:85
  172.4 3.3 %select_add_fusion.4 = f32[1024,768]{1,0:T(8,128)S(1)} fusion(f32[1024,768]{1,0:T(8,128)S(1)} %get-tuple-element.319, bf16[512,1024]{1,0:T(8,128)(2,1)} %get-tuple-element.286, pred[]{:T(512)S(6)} %compare.3, bf16[8,512,768]{2,1,0:T(8,128)(2,1)} %get-tuple-element.331, s32[]{:T(128)} %get-tuple-element.318), kind=kOutput, calls=%fused_computation.4.clone.1 | convolution fusion | flops 806879232 | bytes 8126977 | tf_op jit(solution)/shard_map/while/body/eval_jaxpr/dot_general | solution.py:91
  175.7 3.9 %convert_reduce_fusion.2 = (f32[1024]{0:T(1024)S(1)}, bf16[512,1024]{1,0:T(8,128)(2,1)}) fusion(f32[512]{0:T(512)S(1)} %bitcast.34, bf16[1024,768]{1,0:T(8,128)(2,1)} %get-tuple-element.332, bf16[8,512,768]{2,1,0:T(8,128)(2,1)} %get-tuple-element.331, s32[]{:T(128)} %get-tuple-element.318, f32[1024]{0:T(1024)S(1)} %get-tuple-element.330), kind=kOutput, calls=%fused_computation.5.clone.1 | convolution fusion | flops 808975360 | bytes 3418624 | tf_op jit(solution)/shard_map/while/body/eval_jaxpr/dot_general | solution.py:85
  179.6 3.3 %select_add_fusion.4 = f32[1024,768]{1,0:T(8,128)S(1)} fusion(f32[1024,768]{1,0:T(8,128)S(1)} %get-tuple-element.319, bf16[512,1024]{1,0:T(8,128)(2,1)} %get-tuple-element.286, pred[]{:T(512)S(6)} %compare.3, bf16[8,512,768]{2,1,0:T(8,128)(2,1)} %get-tuple-element.331, s32[]{:T(128)} %get-tuple-element.318), kind=kOutput, calls=%fused_computation.4.clone.1 | convolution fusion | flops 806879232 | bytes 8126977 | tf_op jit(solution)/shard_map/while/body/eval_jaxpr/dot_general | solution.py:91
  185.4 50.3 %all_to_all.15 = f32[16,64,769]{2,1,0:T(8,128)} all-to-all(f32[16,64,769]{2,1,0:T(8,128)S(1)} %pad_maximum_fusion), channel_id=1, replica_groups=mesh['blk'=8,'rows'=16] {'rows'}, dimensions={0} | all-to-all | bytes 6299648 | tf_op jit(solution)/shard_map/all_to_all | solution.py:29
  238.9 33.1 %all-gather.2.cloned.1.call-done = f32[1024,769]{1,0:T(8,128)} async-done(((f32[64,769]{1,0:T(8,128)}), f32[1024,769]{1,0:T(8,128)}) %all-gather.2.cloned.1.call-update) | async-done | bytes 3149840 | tf_op jit(solution)/shard_map/all_gather | solution.py:50
  272.0 3.8 %split.18 = f32[1024,768]{1,0:T(8,128)} slice(f32[1024,769]{1,0:T(8,128)} %all-gather.2.cloned.1.call-done), slice={[0:1024], [0:768]} | slice | bytes 6291456 | tf_op jit(solution)/shard_map/split | solution.py:51
  (54 shorter events, 16.9 us)
Async XLA Ops:
  12.9 8.6 %copy-start = (bf16[1024,768]{1,0:T(8,128)(2,1)S(1)}, bf16[1024,768]{1,0:T(8,128)(2,1)}, u32[]{:S(2)}) copy-start(bf16[1024,768]{1,0:T(8,128)(2,1)} %param.8) | copy-start | bytes 4718596
  12.9 81.2 %all-to-all-start = ((bf16[8,512,768]{2,1,0:T(8,128)(2,1)}), bf16[8,512,768]{2,1,0:T(8,128)(2,1)}, u32[]{:S(2)}, u32[]{:S(2)}) async-start(bf16[8,512,768]{2,1,0:T(8,128)(2,1)} %stack.2), calls=%async_computation | async-start | bytes 12582912 | tf_op jit(solution)/shard_map/all_to_all | solution.py:75
  21.6 72.6 %copy-start.2 = (f32[1024]{0:T(1024)S(1)}, f32[1024]{0:T(1024)}, u32[]{:S(2)}) copy-start(f32[1024]{0:T(1024)} %param.9) | copy-start | bytes 12292
  113.4 4.5 %copy-start.1 = (bf16[1024,768]{1,0:T(8,128)(2,1)}, bf16[1024,768]{1,0:T(8,128)(2,1)S(1)}, u32[]{:S(2)}) copy-start(bf16[1024,768]{1,0:T(8,128)(2,1)S(1)} %get-tuple-element.340) | copy-start | bytes 4718596
  114.2 10.8 %all-to-all-start.1 = ((f32[8,8,512]{2,1,0:T(8,128)}), f32[8,8,512]{2,1,0:T(8,128)S(1)}, u32[]{:S(2)}, u32[]{:S(2)}) async-start(f32[8,8,512]{2,1,0:T(8,128)} %broadcast_in_dim.31), calls=%async_computation.1 | async-start | bytes 262144 | tf_op jit(solution)/shard_map/all_to_all | solution.py:13
  117.9 154.1 %all-gather.2.cloned.1.call-start = ((), (), s32[]{:S(2)}) async-start(), calls=%async_computation.3 | async-start | bytes 3899392 | tf_op jit(solution)/shard_map/all_gather | solution.py:50
Sparse Core Ops, SparseCore 0:
  239.0 32.9 all-gather.1
